TPU v7x, 128 devices: a whole 4x4x4 slice. The times are simulated.
128 devices in a mesh: seq: 16 (over x, z), head: 8 (over y, core).
Axes of the slice: x: 4, y: 4, z: 4, core: 2. Of those that a mesh axis runs over, the one named last changes fastest.
Arguments:
- context: bfloat16 [8, 8192, 1024], P('head', 'seq'), may hold values from -6 to 6
- latents: bfloat16 [8, 1024, 1024], P('head'), may hold values from -6 to 6
- offsets: int32 [8], P('head'), may hold values from 0 to 7168
- query_gain: float32 [1024], replicated, may hold values from 0.1 to 1.9
- key_gain: float32 [1024], replicated, may hold values from 0.1 to 1.9
- layer_gain: float32 [2, 1024], replicated, may hold values from 0.1 to 1.9
- cross_query: bfloat16 [1024, 1024], P(('seq', 'head')), may hold values from -0.25 to 0.25
- cross_key: bfloat16 [1024, 1024], P(('seq', 'head')), may hold values from -0.25 to 0.25
- cross_value: bfloat16 [1024, 1024], P(('seq', 'head')), may hold values from -0.1875 to 0.1875
- cross_out: bfloat16 [1024, 1024], P(('seq', 'head')), may hold values from -0.1875 to 0.1875
- layer_qkv: bfloat16 [2, 1024, 3072], P(None, ('seq', 'head')), may hold values from -0.25 to 0.25
- layer_out: bfloat16 [2, 1024, 1024], P(None, ('seq', 'head')), may hold values from -0.1875 to 0.1875
Outputs:
- latent_out: bfloat16 [8, 1024, 1024], P('head', 'seq')
Inputs may be any that keep to these rules, and one draw needn't show every extreme that they name: Latent i of row b stands at context position offsets[b] + i.
All inputs are finite; a program needn't handle non-finite values.
Results may differ from a plain program's by a relative error of at most 0.013.
Values may be sent and summed in bfloat16 or wider, within the bound.
A program may use at most 128 MiB of HBM per device.

v0:
```python
import jax
import jax.numpy as jnp
from jax import lax
from jax.sharding import PartitionSpec as P

H = 16
EPSILON = 1e-06
NEGATIVE = -1e30


def rows_first(arrays, axis, dims):
    turned = [jnp.moveaxis(a, dim, 0) for a, dim in zip(arrays, dims)]
    widths = [t[0].size for t in turned]
    both = jnp.concatenate([t.reshape(-1, w) for t, w in zip(turned, widths)], axis=1)
    out = lax.all_gather(both, axis, axis=0, tiled=True)
    parts = jnp.split(out, [sum(widths[:k]) for k in range(1, len(widths))], axis=1)
    return tuple(
        (
            jnp.moveaxis(b.reshape(-1, *t.shape[1:]), 0, dim)
            for b, t, dim in zip(parts, turned, dims)
        )
    )


def rms_norm(value_matrix, gain):
    value_matrix = value_matrix.astype(jnp.float32)
    scale = lax.rsqrt(jnp.mean(value_matrix * value_matrix, axis=-1, keepdims=True) + EPSILON)
    return (value_matrix * scale * gain).astype(jnp.bfloat16)


def project(left, weight):
    return jnp.einsum("...k,kn->...n", left, weight, preferred_element_type=jnp.float32)


def block_scores(query_row_block, key_rows, query_pos, key_base, start, key_span, scale):
    key_tile = lax.dynamic_slice_in_dim(key_rows, start, key_span, 0)
    score_matrix = (
        jnp.einsum("oqi,cqi->qoc", query_row_block, key_tile, preferred_element_type=jnp.float32)
        * scale
    )
    key_pos = key_base + start + jnp.arange(key_span, dtype=jnp.int32)
    valid = key_pos[None, None, :] <= query_pos[None, :, None]
    return (jnp.where(valid, score_matrix, NEGATIVE), valid)


def causal_top(query_row_block, key_rows, query_pos, last_pos, key_base, key_span, scale):

    def advance(index, best):
        start = index * key_span

        def compute(kept):
            score_matrix, valid = block_scores(
                query_row_block, key_rows, query_pos, key_base, start, key_span, scale
            )
            return jnp.maximum(kept, jnp.max(score_matrix, axis=2))

        result = lax.cond(key_base + start <= last_pos, compute, lambda kept: kept, best)
        return result

    initial = jnp.full((query_row_block.shape[1], query_row_block.shape[0]), NEGATIVE, jnp.float32)
    return lax.fori_loop(0, key_rows.shape[0] // key_span, advance, initial)


def causal_sums(
    query_row_block, key_rows, value_rows, row_top, query_pos, last_pos, key_base, key_span, scale
):

    def advance(index, carry):
        start = index * key_span

        def compute(kept):
            numerator_sum, denom = kept
            score_matrix, valid = block_scores(
                query_row_block, key_rows, query_pos, key_base, start, key_span, scale
            )
            probability_rows = jnp.where(
                valid, jnp.exp(score_matrix - row_top[:, :, None]), 0.0
            ).astype(jnp.bfloat16)
            value_tile = lax.dynamic_slice_in_dim(value_rows, start, key_span, 0)
            numerator_sum = numerator_sum + jnp.einsum(
                "ycv,vys->cys", probability_rows, value_tile, preferred_element_type=jnp.float32
            )
            denom = denom + jnp.transpose(jnp.sum(probability_rows.astype(jnp.float32), axis=2))
            return (numerator_sum, denom)

        result = lax.cond(key_base + start <= last_pos, compute, lambda kept: kept, carry)
        return result

    count, heads, head_width = query_row_block.shape
    initial = (
        jnp.zeros((count, heads, head_width), jnp.float32),
        jnp.zeros((count, heads), jnp.float32),
    )
    return lax.fori_loop(0, key_rows.shape[0] // key_span, advance, initial)


def latent_attention(piece):
    count = piece.shape[1]
    head_width = piece.shape[-1]
    query_matrix = piece[:, :, 0]
    key_matrix = piece[:, :, 1]
    value_matrix = piece[:, :, 2]
    score_matrix = jnp.einsum(
        "bmhd,bkhd->bhmk", query_matrix, key_matrix, preferred_element_type=jnp.float32
    ) * head_width ** (-0.5)
    positions = jnp.arange(count, dtype=jnp.int32)
    valid = positions[None, :] <= positions[:, None]
    score_matrix = jnp.where(valid, score_matrix, NEGATIVE)
    row_top = jnp.max(score_matrix, axis=3, keepdims=True)
    probability_rows = jnp.where(valid, jnp.exp(score_matrix - row_top), 0.0).astype(jnp.bfloat16)
    denom = jnp.sum(probability_rows.astype(jnp.float32), axis=3)
    numerator_sum = jnp.einsum(
        "bhmk,bkhd->bmhd", probability_rows, value_matrix, preferred_element_type=jnp.float32
    )
    return (numerator_sum / jnp.transpose(denom, (0, 2, 1))[:, :, :, None]).astype(jnp.bfloat16)


def per_device(
    context,
    latents,
    offsets,
    query_gain,
    key_gain,
    layer_gain,
    cross_query,
    cross_key,
    cross_value,
    cross_out,
    layer_qkv,
    layer_out,
):
    batch, ctx_len, width = context.shape
    latent_count = latents.shape[1]
    heads = H
    head_width = width // heads
    groups = lax.axis_size("seq")
    local_rows = latent_count // groups
    group_heads = heads // groups
    seq_index = lax.axis_index("seq")
    scale = head_width ** (-0.5)
    gathered = rows_first(
        (cross_query, cross_key, cross_value, cross_out, layer_qkv, layer_out),
        ("seq", "head"),
        (0, 0, 0, 0, 1, 1),
    )
    normed_latents = rms_norm(latents, query_gain)
    query_matrix = project(normed_latents, gathered[0])
    query_matrix = query_matrix.astype(jnp.bfloat16)
    normed_context = rms_norm(context, key_gain)
    key_matrix = project(normed_context, gathered[1])
    value_matrix = project(normed_context, gathered[2])
    key_matrix = key_matrix.astype(jnp.bfloat16).reshape(batch, ctx_len, heads, head_width)
    value_matrix = value_matrix.astype(jnp.bfloat16).reshape(batch, ctx_len, heads, head_width)
    query_head_rows = query_matrix.reshape(batch, latent_count, heads, head_width)
    query_pos = offsets[:, None] + jnp.arange(latent_count, dtype=jnp.int32)[None, :]
    last_pos = offsets + (latent_count - 1)
    key_groups, value_groups = (
        lax.all_to_all(key_matrix, "seq", split_axis=2, concat_axis=1, tiled=True),
        lax.all_to_all(value_matrix, "seq", split_axis=2, concat_axis=1, tiled=True),
    )
    query_groups = lax.dynamic_slice_in_dim(
        query_head_rows, seq_index * group_heads, group_heads, 2
    )
    total_len = key_groups.shape[1]
    key_span = max(min(total_len, 512), total_len // 16)
    row_top = causal_top(
        query_groups[0], key_groups[0], query_pos[0], last_pos[0], 0, key_span, scale
    )
    numerator_sum, denom = causal_sums(
        query_groups[0],
        key_groups[0],
        value_groups[0],
        row_top,
        query_pos[0],
        last_pos[0],
        0,
        key_span,
        scale,
    )
    results = [(numerator_sum / denom[:, :, None]).astype(jnp.bfloat16)]
    attended = lax.all_to_all(
        jnp.stack(results), "seq", split_axis=1, concat_axis=2, tiled=True
    ).reshape(batch, local_rows, width)
    latents_own = lax.dynamic_slice_in_dim(latents, seq_index * local_rows, local_rows, 1)
    update = project(attended, gathered[3])
    hidden = (latents_own.astype(jnp.float32) + update).astype(jnp.bfloat16)
    for layer in range(layer_qkv.shape[0]):
        normed = rms_norm(hidden, layer_gain[layer])
        qkv = project(normed, gathered[4][layer])
        grouped = qkv.astype(jnp.bfloat16).reshape(batch, local_rows, 3, heads, head_width)
        mixed = latent_attention(
            lax.all_to_all(grouped, "seq", split_axis=3, concat_axis=1, tiled=True)
        )
        merged = lax.all_to_all(mixed, "seq", split_axis=1, concat_axis=2, tiled=True).reshape(
            batch, local_rows, width
        )
        update = project(merged, gathered[5][layer])
        hidden = (hidden.astype(jnp.float32) + update).astype(jnp.bfloat16)
    return hidden


def solution(mesh):
    return jax.shard_map(
        per_device,
        mesh=mesh,
        in_specs=(
            P("head", "seq", None),
            P("head", None, None),
            P("head"),
            P(),
            P(),
            P(),
            P(("seq", "head"), None),
            P(("seq", "head"), None),
            P(("seq", "head"), None),
            P(("seq", "head"), None),
            P(None, ("seq", "head"), None),
            P(None, ("seq", "head"), None),
        ),
        out_specs=P("head", "seq", None),
        check_vma=False,
    )
```

profile of v0, /device:TPU:8, one launch (start us, length us, event | category | flops | bytes accessed | tf_op | source)
XLA Modules:
  0.0 371.7 jit_solution(11216655208212201364)
XLA Ops:
  13.3 93.9 %all-gather.2.cloned.1.call-done = bf16[1024,12288]{1,0:T(8,128)(2,1)} async-done(((bf16[8,12288]{1,0:T(8,128)(2,1)}), bf16[1024,12288]{1,0:T(8,128)(2,1)}) %all-gather.2.cloned.1.call-update) | async-done | bytes 25165840 | tf_op jit(solution)/shard_map/all_gather | solution.py:15
  107.2 3.2 fusion.54
  111.8 5.1 %all-to-all-start.1 = ((bf16[1,512,16,64]{1,3,0,2:T(8,128)(2,1)}), bf16[1,512,16,64]{1,3,0,2:T(8,128)(2,1)S(1)}, u32[]{:S(2)}, u32[]{:S(2)}) async-start(bf16[1,512,16,64]{1,3,0,2:T(8,128)(2,1)} %bitcast.25), calls=%async_computation.1 | async-start | bytes 2097152 | tf_op jit(solution)/shard_map/all_to_all | solution.py:158
  116.9 2.9 fusion.51
  121.2 14.0 %all-to-all-done.1 = bf16[1,512,16,64]{1,3,0,2:T(8,128)(2,1)S(1)} async-done(((bf16[1,512,16,64]{1,3,0,2:T(8,128)(2,1)}), bf16[1,512,16,64]{1,3,0,2:T(8,128)(2,1)S(1)}, u32[]{:S(2)}, u32[]{:S(2)}) %all-to-all-start.1) | async-done | bytes 1048608 | tf_op jit(solution)/shard_map/all_to_all | solution.py:158
  135.1 3.8 %all-to-all-start = ((bf16[1,512,16,64]{1,3,0,2:T(8,128)(2,1)}), bf16[1,512,16,64]{1,3,0,2:T(8,128)(2,1)S(1)}, u32[]{:S(2)}, u32[]{:S(2)}) async-start(bf16[1,512,16,64]{1,3,0,2:T(8,128)(2,1)} %bitcast.21), calls=%async_computation | async-start | bytes 2097152 | tf_op jit(solution)/shard_map/all_to_all | solution.py:159
  139.0 2.1 fusion.22
  141.7 4.8 %fusion.46 = bf16[1024,1024]{0,1:T(8,128)(2,1)S(1)} fusion(bf16[1024,12288]{1,0:T(8,128)(2,1)} %all-gather.2.cloned.1.call-done, bf16[1,1024,1024]{2,1,0:T(8,128)(2,1)} %param.21, f32[1024]{0:T(1024)S(1)} %copy-done.4, f32[1024]{0:T(1024)S(1)} %add_rsqrt_fusion), kind=kOutput, calls=%fused_computation.67 | convolution fusion | flops 2152726528 | bytes 6299648 | tf_op jit(solution)/shard_map/...k,kn->...n/dot_general | solution.py:32
  148.5 6.2 %all-to-all-done = bf16[1,512,16,64]{1,3,0,2:T(8,128)(2,1)S(1)} async-done(((bf16[1,512,16,64]{1,3,0,2:T(8,128)(2,1)}), bf16[1,512,16,64]{1,3,0,2:T(8,128)(2,1)S(1)}, u32[]{:S(2)}, u32[]{:S(2)}) %all-to-all-start) | async-done | bytes 1048608 | tf_op jit(solution)/shard_map/all_to_all | solution.py:159
  155.9 33.2 %while.33 = (s32[]{:T(128)}, f32[1,1024]{1,0:T(1,128)S(1)}, s32[]{:T(128)}, bf16[8192,1,64]{0,2,1:T(8,128)(2,1)}, bf16[1024,1,64]{0,2,1:T(8,128)(2,1)S(1)}, /*index=5*/s32[]{:T(128)}, s32[]{:T(128)}, s32[]{:T(128)}) while((s32[]{:T(128)}, f32[1,1024]{1,0:T(1,128)S(1)}, s32[]{:T(128)}, bf16[8192,1,64]{0,2,1:T(8,128)(2,1)}, ...), condition=%wide.region_6.7_spmd.clone, body=%wide.region_2.6_spmd.clone.sunk | while | flops 69207552 | bytes 233685 | solution.py:61
  155.9 2.0 conditional.6
  158.0 2.0 conditional.6
  160.1 2.0 conditional.6
  162.2 2.0 conditional.6
  164.3 2.0 conditional.6
  166.3 2.0 conditional.6
  168.4 2.0 conditional.6
  170.5 2.0 conditional.6
  172.6 2.0 conditional.6
  174.6 2.0 conditional.6
  176.7 2.0 conditional.6
  178.8 2.0 conditional.6
  180.9 2.0 conditional.6
  182.9 2.0 conditional.6
  185.0 2.0 conditional.6
  187.1 2.0 conditional.6
  189.2 43.4 %while.34 = (s32[]{:T(128)}, f32[1024,1,64]{0,2,1:T(8,128)S(1)}, f32[1024,1]{0,1:T(1,128)S(1)}, s32[]{:T(128)}, bf16[8192,1,64]{0,2,1:T(8,128)(2,1)S(1)}, /*inde...) while((s32[]{:T(128)}, f32[1024,1,64]{0,2,1:T(8,128)S(1)}, ...), condition=%wide.region_11.12_spmd.clone, body=%wide.region_7.11_spmd.clone.sunk | while | flops 138479104 | bytes 2924841 | solution.py:94
  189.2 2.7 conditional.7
  191.9 2.7 conditional.7
  192.6 1.6 convert_reduce_fusion
  194.7 2.7 conditional.7
  195.4 1.6 convert_reduce_fusion
  197.4 2.7 conditional.7
  200.1 2.7 conditional.7
  202.8 2.7 conditional.7
  205.5 2.7 conditional.7
  208.2 2.7 conditional.7
  210.9 2.7 conditional.7
  213.6 2.7 conditional.7
  216.4 2.7 conditional.7
  217.1 1.6 convert_reduce_fusion
  219.1 2.7 conditional.7
  221.8 2.7 conditional.7
  224.5 2.7 conditional.7
  227.2 2.7 conditional.7
  227.9 1.6 convert_reduce_fusion
  229.9 2.7 conditional.7
  233.6 2.2 reduce.16
  236.7 3.8 %all-to-all-start.2 = ((bf16[16,2,2048]{2,1,0:T(2,128)(2,1)}), bf16[16,2,2048]{2,1,0:T(2,128)(2,1)S(1)}, u32[]{:S(2)}, u32[]{:S(2)}) async-start(bf16[16,2,2048]{2,1,0:T(2,128)(2,1)} %reshape.299), calls=%async_computation.2 | async-start | bytes 262144 | tf_op jit(solution)/shard_map/all_to_all | solution.py:181
  240.5 10.7 %split.28 = bf16[1024,6144]{1,0:T(8,128)(2,1)} slice(bf16[1024,12288]{1,0:T(8,128)(2,1)} %all-gather.2.cloned.1.call-done), slice={[0:1024], [4096:10240]} | slice | bytes 25165824 | tf_op jit(solution)/shard_map/split | solution.py:16
  251.2 16.6 %copy.91 = bf16[1024,6144]{0,1:T(8,128)(2,1)} copy(bf16[1024,6144]{1,0:T(8,128)(2,1)} %split.28) | data formatting | bytes 25165824
  269.2 2.2 multiply_reduce_fusion.1
  271.4 4.8 %fusion.25 = bf16[64,3072]{1,0:T(8,128)(2,1)S(1)} fusion(bf16[2,1024,3072]{1,2,0:T(8,128)(2,1)} %bitcast.260, f32[1,64,1024]{2,1,0:T(8,128)S(1)} %get-tuple-element.412, f32[1024]{0:T(1024)S(1)} %bitcast.285, f32[64]{0:T(128)S(1)} %add_rsqrt_fusion.3), kind=kOutput, calls=%fused_computation.43 | convolution fusion | flops 403046400 | bytes 6951168 | tf_op jit(solution)/shard_map/...k,kn->...n/dot_general | solution.py:32
  278.1 16.0 %all_to_all.111 = bf16[16,2,6144]{2,1,0:T(2,128)(2,1)S(1)} all-to-all(bf16[16,2,6144]{2,1,0:T(2,128)(2,1)S(1)} %reshape.301), channel_id=1, replica_groups=mesh['seq'=16,'head'=8] {'seq'}, dimensions={0} | all-to-all | bytes 786432 | tf_op jit(solution)/shard_map/all_to_all | solution.py:192
  298.0 2.2 reduce.17
  301.1 3.8 %all-to-all-start.4 = ((bf16[16,2,2048]{2,1,0:T(2,128)(2,1)}), bf16[16,2,2048]{2,1,0:T(2,128)(2,1)S(1)}, u32[]{:S(2)}, u32[]{:S(2)}) async-start(bf16[16,2,2048]{2,1,0:T(2,128)(2,1)} %reshape.303), calls=%async_computation.4 | async-start | bytes 262144 | tf_op jit(solution)/shard_map/all_to_all | solution.py:194
  305.0 4.7 %split.29 = bf16[1024,2048]{1,0:T(8,128)(2,1)} slice(bf16[1024,12288]{1,0:T(8,128)(2,1)} %all-gather.2.cloned.1.call-done), slice={[0:1024], [10240:12288]} | slice | bytes 8388608 | tf_op jit(solution)/shard_map/split | solution.py:16
  309.7 6.4 %copy.92 = bf16[1024,2048]{0,1:T(8,128)(2,1)} copy(bf16[1024,2048]{1,0:T(8,128)(2,1)} %split.29) | data formatting | bytes 8388608
  317.5 2.5 multiply_reduce_fusion
  320.0 4.8 %fusion.26 = bf16[64,3072]{1,0:T(8,128)(2,1)S(1)} fusion(bf16[2,1024,3072]{1,2,0:T(8,128)(2,1)} %bitcast.261, f32[1,64,1024]{2,1,0:T(8,128)S(1)} %get-tuple-element.416, f32[1024]{0:T(1024)S(1)} %bitcast.284, f32[64]{0:T(128)S(1)} %add_rsqrt_fusion.2), kind=kOutput, calls=%fused_computation.44 | convolution fusion | flops 403046400 | bytes 6951168 | tf_op jit(solution)/shard_map/...k,kn->...n/dot_general | solution.py:32
  326.7 16.0 %all_to_all.112 = bf16[16,2,6144]{2,1,0:T(2,128)(2,1)S(1)} all-to-all(bf16[16,2,6144]{2,1,0:T(2,128)(2,1)S(1)} %reshape.305), channel_id=1, replica_groups=mesh['seq'=16,'head'=8] {'seq'}, dimensions={0} | all-to-all | bytes 786432 | tf_op jit(solution)/shard_map/all_to_all | solution.py:192
  346.6 2.2 reduce.18
  349.1 11.4 %all_to_all.113 = bf16[16,2,2048]{2,1,0:T(2,128)(2,1)S(1)} all-to-all(bf16[16,2,2048]{2,1,0:T(2,128)(2,1)S(1)} %reshape.307), channel_id=1, replica_groups=mesh['seq'=16,'head'=8] {'seq'}, dimensions={0} | all-to-all | bytes 262144 | tf_op jit(solution)/shard_map/all_to_all | solution.py:194
  361.9 3.0 fusion.75
  (251 shorter events, 98.4 us)
Async XLA Ops:
  6.5 100.6 %all-gather.2.cloned.1.call-start = ((), (), s32[]{:S(2)}) async-start(), calls=%async_computation.7 | async-start | bytes 25362432 | tf_op jit(solution)/shard_map/all_gather | solution.py:15
  11.1 0.7 copy-start.1
  110.4 6.5 %copy-start = (bf16[1,512,1024]{2,1,0:T(8,128)(2,1)S(1)}, bf16[1,512,1024]{2,1,0:T(8,128)(2,1)}, u32[]{:S(2)}) copy-start(bf16[1,512,1024]{2,1,0:T(8,128)(2,1)} %param.20) | copy-start | bytes 3145732
  110.4 6.5 %copy-start.3 = (f32[1024]{0:T(1024)S(1)}, f32[1024]{0:T(1024)}, u32[]{:S(2)}) copy-start(f32[1024]{0:T(1024)} %param.24) | copy-start | bytes 12292
  111.8 23.3 %all-to-all-start.1 = ((bf16[1,512,16,64]{1,3,0,2:T(8,128)(2,1)}), bf16[1,512,16,64]{1,3,0,2:T(8,128)(2,1)S(1)}, u32[]{:S(2)}, u32[]{:S(2)}) async-start(bf16[1,512,16,64]{1,3,0,2:T(8,128)(2,1)} %bitcast.25), calls=%async_computation.1 | async-start | bytes 2097152 | tf_op jit(solution)/shard_map/all_to_all | solution.py:158
  119.8 21.9 %copy-start.4 = (f32[1024]{0:T(1024)S(1)}, f32[1024]{0:T(1024)}, u32[]{:S(2)}) copy-start(f32[1024]{0:T(1024)} %param.23) | copy-start | bytes 12292
  135.1 19.6 %all-to-all-start = ((bf16[1,512,16,64]{1,3,0,2:T(8,128)(2,1)}), bf16[1,512,16,64]{1,3,0,2:T(8,128)(2,1)S(1)}, u32[]{:S(2)}, u32[]{:S(2)}) async-start(bf16[1,512,16,64]{1,3,0,2:T(8,128)(2,1)} %bitcast.21), calls=%async_computation | async-start | bytes 2097152 | tf_op jit(solution)/shard_map/all_to_all | solution.py:159
  189.2 51.3 %copy-start.2 = (f32[2,1024]{1,0:T(2,128)S(1)}, f32[2,1024]{1,0:T(2,128)}, u32[]{:S(2)}) copy-start(f32[2,1024]{1,0:T(2,128)} %param.25) | copy-start | bytes 24580
  236.7 31.1 %all-to-all-start.2 = ((bf16[16,2,2048]{2,1,0:T(2,128)(2,1)}), bf16[16,2,2048]{2,1,0:T(2,128)(2,1)S(1)}, u32[]{:S(2)}, u32[]{:S(2)}) async-start(bf16[16,2,2048]{2,1,0:T(2,128)(2,1)} %reshape.299), calls=%async_computation.2 | async-start | bytes 262144 | tf_op jit(solution)/shard_map/all_to_all | solution.py:181
  301.1 14.9 %all-to-all-start.4 = ((bf16[16,2,2048]{2,1,0:T(2,128)(2,1)}), bf16[16,2,2048]{2,1,0:T(2,128)(2,1)S(1)}, u32[]{:S(2)}, u32[]{:S(2)}) async-start(bf16[16,2,2048]{2,1,0:T(2,128)(2,1)} %reshape.303), calls=%async_computation.4 | async-start | bytes 262144 | tf_op jit(solution)/shard_map/all_to_all | solution.py:194
Sparse Core Ops, SparseCore 0:
  11.9 95.2 all-gather.1
where the time goes:
time: 375 us; the launch traced here: 372 us
  waiting for transfers between devices  114 us (30%)
  matrix products  82.9 us (22%)
  local copies, waits for them, and re-layouts  64.5 us (17%)
  blocking collectives  43.4 us (12%)
  other arithmetic  33 us (9%)
  starting transfers between devices  16.5 us (4%)
  between operations  14.6 us (4%)
    all_gather x1, waiting for transfers between devices, rows_first(): out = lax.all_gather(both, axis, axis=0, tiled=True)  93.9 us
    dot_general x32, matrix products, block_scores(): jnp.einsum('oqi,cqi->qoc', query_row_block, key_tile, preferred_element_t...  47.2 us
    unnamed x28, local copies, waits for them, and re-layouts  33.1 us
    all_to_all x2, blocking collectives, per_device(): lax.all_to_all(grouped, 'seq', split_axis=3, concat_axis=1, tiled=True)  32 us
    dot_general x8, matrix products, project(): jnp.einsum('...k,kn->...n', left, weight, preferred_element_type=jnp.floa...  28.2 us
    add x32, other arithmetic, per_device(): offsets[:, None] + jnp.arange(latent_count, dtype=jnp.int32)[None, :]  20.9 us
    split x2, local copies, waits for them, and re-layouts, rows_first(): jnp.split(out, [sum(widths[:k]) for k in range(1, len(widths))], axis=1)  15.4 us
    all_to_all x1, waiting for transfers between devices, per_device(): lax.all_to_all(key_matrix, 'seq', split_axis=2, concat_axis=1, tiled=True)  14 us
  transfers between devices with their start and end apart: 5, of which 3 were waited for; matrix products, arithmetic and copies ran while one was open for 14% of the time, Pallas kernels for 0%

commit v1 on v0

--- a/solution.py
+++ b/solution.py
@@ -12,7 +12,9 @@
     turned = [jnp.moveaxis(a, dim, 0) for a, dim in zip(arrays, dims)]
     widths = [t[0].size for t in turned]
     both = jnp.concatenate([t.reshape(-1, w) for t, w in zip(turned, widths)], axis=1)
-    out = lax.all_gather(both, axis, axis=0, tiled=True)
+    out = jnp.concatenate(
+        lax.all_to_all(jnp.stack([both] * lax.axis_size(axis)), axis, 0, 0), axis=0
+    )
     parts = jnp.split(out, [sum(widths[:k]) for k in range(1, len(widths))], axis=1)
     return tuple(
         (

time: 375 us -> 664 us (1.77)
  the two profiles are of different devices: /device:TPU:8 before, /device:TPU:16 now
where the time goes in v1:
time: 664 us; the launch traced here: 658 us
  waiting for transfers between devices  377 us (57%)
  local copies, waits for them, and re-layouts  72.7 us (11%)
  matrix products  69.4 us (10%)
  starting transfers between devices  58.2 us (9%)
  blocking collectives  44.9 us (7%)
  other arithmetic  31.7 us (5%)
    all_to_all x1, waiting for transfers between devices, rows_first(): lax.all_to_all(jnp.stack([both] * lax.axis_size(axis)), axis, 0, 0)  364 us
    split x4, local copies, waits for them, and re-layouts, rows_first(): jnp.split(out, [sum(widths[:k]) for k in range(1, len(widths))], axis=1)  38.4 us
    dot_general x32, matrix products, block_scores(): jnp.einsum('oqi,cqi->qoc', query_row_block, key_tile, preferred_element_t...  34 us
    all_to_all x2, blocking collectives, per_device(): lax.all_to_all(grouped, 'seq', split_axis=3, concat_axis=1, tiled=True)  33.6 us
    all_to_all x1, starting transfers between devices, per_device(): lax.all_to_all(key_matrix, 'seq', split_axis=2, concat_axis=1, tiled=True)  31.3 us
    dot_general x8, matrix products, project(): jnp.einsum('...k,kn->...n', left, weight, preferred_element_type=jnp.floa...  27.9 us
    add x32, other arithmetic, per_device(): offsets[:, None] + jnp.arange(latent_count, dtype=jnp.int32)[None, :]  20.9 us
  transfers between devices with their start and end apart: 5, of which 2 were waited for; matrix products, arithmetic and copies ran while one was open for 11% of the time, Pallas kernels for 0%

profile of v1, /device:TPU:16, one launch (start us, length us, event | category | flops | bytes accessed | tf_op | source)
XLA Modules:
  0.0 658.1 jit_solution(10617318229582156548)
XLA Ops:
  4.5 8.7 %stack.4 = bf16[128,8,12288]{2,1,0:T(8,128)(2,1)} broadcast(bf16[8,12288]{1,0:T(8,128)(2,1)S(1)} %constant_dynamic-update-slice_fusion), dimensions={1,2} | broadcast | bytes 25362432 | tf_op jit(solution)/shard_map/stack | solution.py:16
  13.2 10.7 %all-to-all-start = ((bf16[128,8,12288]{2,1,0:T(8,128)(2,1)}), bf16[128,8,12288]{2,1,0:T(8,128)(2,1)}, u32[]{:S(2)}, u32[]{:S(2)}) async-start(bf16[128,8,12288]{2,1,0:T(8,128)(2,1)} %stack.4), calls=%async_computation | async-start | bytes 50331648 | tf_op jit(solution)/shard_map/all_to_all | solution.py:16
  24.3 364.0 %all-to-all-done = bf16[128,8,12288]{2,1,0:T(8,128)(2,1)} async-done(((bf16[128,8,12288]{2,1,0:T(8,128)(2,1)}), bf16[128,8,12288]{2,1,0:T(8,128)(2,1)}, u32[]{:S(2)}, u32[]{:S(2)}) %all-to-all-start) | async-done | bytes 25165856 | tf_op jit(solution)/shard_map/all_to_all | solution.py:16
  388.2 2.9 fusion.54
  391.1 1.4 copy.82
  392.5 31.3 %all-to-all-start.2 = ((bf16[1,512,16,64]{1,3,0,2:T(8,128)(2,1)}), bf16[1,512,16,64]{1,3,0,2:T(8,128)(2,1)S(1)}, u32[]{:S(2)}, u32[]{:S(2)}) async-start(bf16[1,512,16,64]{1,3,0,2:T(8,128)(2,1)} %bitcast.26), calls=%async_computation.2 | async-start | bytes 2097152 | tf_op jit(solution)/shard_map/all_to_all | solution.py:160
  423.8 2.9 fusion.51
  426.7 1.3 copy.79
  428.0 13.1 %all-to-all-done.2 = bf16[1,512,16,64]{1,3,0,2:T(8,128)(2,1)S(1)} async-done(((bf16[1,512,16,64]{1,3,0,2:T(8,128)(2,1)}), bf16[1,512,16,64]{1,3,0,2:T(8,128)(2,1)S(1)}, u32[]{:S(2)}, u32[]{:S(2)}) %all-to-all-start.2) | async-done | bytes 1048608 | tf_op jit(solution)/shard_map/all_to_all | solution.py:160
  441.2 4.1 all-to-all-start.1
  445.3 2.1 fusion.22
  448.0 4.8 fusion.46
  454.0 19.9 %while.33 = (s32[]{:T(128)}, f32[1,1024]{1,0:T(1,128)S(1)}, s32[]{:T(128)}, bf16[8192,1,64]{0,2,1:T(8,128)(2,1)S(1)}, bf16[1024,1,64]{0,2,1:T(8,128)(2,1)S(1)}, /*index=5*/s32[]{:T(128)}, s32[]{:T(128)}, s32[]{:T(128)}) while((s32[]{:T(128)}, f32[1,1024]{1,0:T(1,128)S(1)}, s32[]{:T(128)}, bf16[8192,1,64]{0,2,1:T(8,128)(2,1)S(1)}, ...), condition=%wide.region_6.7_spmd.clone, body=%wide.region_2.6_spmd.clone.sunk | while | flops 69207552 | bytes 233685 | solution.py:63
  470.2 1.2 conditional.6
  476.1 43.5 %while.34 = (s32[]{:T(128)}, f32[1024,1,64]{0,2,1:T(8,128)S(1)}, f32[1024,1]{0,1:T(1,128)S(1)}, s32[]{:T(128)}, bf16[8192,1,64]{0,2,1:T(8,128)(2,1)S(1)}, /*inde...) while((s32[]{:T(128)}, f32[1024,1,64]{0,2,1:T(8,128)S(1)}, ...), condition=%wide.region_11.12_spmd.clone, body=%wide.region_7.11_spmd.clone.sunk | while | flops 138479104 | bytes 2924841 | solution.py:96
  476.1 2.7 conditional.7
  476.8 1.6 convert_reduce_fusion
  478.9 2.7 conditional.7
  479.5 1.6 convert_reduce_fusion
  481.6 2.7 conditional.7
  482.3 1.6 convert_reduce_fusion
  484.3 2.7 conditional.7
  485.0 1.6 convert_reduce_fusion
  487.0 2.7 conditional.7
  487.7 1.6 convert_reduce_fusion
  489.7 2.7 conditional.7
  490.4 1.6 convert_reduce_fusion
  492.4 2.7 conditional.7
  493.1 1.6 convert_reduce_fusion
  495.1 2.7 conditional.7
  495.8 1.6 convert_reduce_fusion
  497.9 2.7 conditional.7
  498.6 1.6 convert_reduce_fusion
  500.6 2.7 conditional.7
  501.3 1.6 convert_reduce_fusion
  503.3 2.7 conditional.7
  504.0 1.6 convert_reduce_fusion
  506.0 2.7 conditional.7
  506.7 1.6 convert_reduce_fusion
  508.7 2.7 conditional.7
  509.4 1.6 convert_reduce_fusion
  511.4 2.7 conditional.7
  512.1 1.6 convert_reduce_fusion
  514.2 2.7 conditional.7
  514.9 1.6 convert_reduce_fusion
  516.9 2.7 conditional.7
  517.6 1.6 convert_reduce_fusion
  520.5 2.2 reduce.16
  523.7 7.4 %all-to-all-start.3 = ((bf16[16,2,2048]{2,1,0:T(2,128)(2,1)}), bf16[16,2,2048]{2,1,0:T(2,128)(2,1)S(1)}, u32[]{:S(2)}, u32[]{:S(2)}) async-start(bf16[16,2,2048]{2,1,0:T(2,128)(2,1)} %reshape.305), calls=%async_computation.3 | async-start | bytes 262144 | tf_op jit(solution)/shard_map/all_to_all | solution.py:183
  531.1 10.7 %split.28 = bf16[1024,6144]{1,0:T(8,128)(2,1)} slice(bf16[1024,12288]{1,0:T(8,128)(2,1)} %bitcast.20), slice={[0:1024], [4096:10240]} | slice | bytes 25165824 | tf_op jit(solution)/shard_map/split | solution.py:18
  541.8 16.6 %copy.88 = bf16[1024,6144]{0,1:T(8,128)(2,1)} copy(bf16[1024,6144]{1,0:T(8,128)(2,1)} %split.28) | data formatting | bytes 25165824 | tf_op jit(solution)/shard_map/split | solution.py:18
  559.9 2.2 multiply_reduce_fusion.1
  562.1 4.8 fusion.25
  568.8 17.3 %all_to_all.116 = bf16[16,2,6144]{2,1,0:T(2,128)(2,1)S(1)} all-to-all(bf16[16,2,6144]{2,1,0:T(2,128)(2,1)S(1)} %reshape.307), channel_id=1, replica_groups=mesh['seq'=16,'head'=8] {'seq'}, dimensions={0} | all-to-all | bytes 786432 | tf_op jit(solution)/shard_map/all_to_all | solution.py:194
  590.0 2.2 reduce.17
  593.1 4.6 all-to-all-start.5
  597.7 4.7 split.29
  602.5 6.4 copy.95
  610.3 2.5 multiply_reduce_fusion
  612.8 4.8 fusion.26
  619.4 16.2 %all_to_all.117 = bf16[16,2,6144]{2,1,0:T(2,128)(2,1)S(1)} all-to-all(bf16[16,2,6144]{2,1,0:T(2,128)(2,1)S(1)} %reshape.311), channel_id=1, replica_groups=mesh['seq'=16,'head'=8] {'seq'}, dimensions={0} | all-to-all | bytes 786432 | tf_op jit(solution)/shard_map/all_to_all | solution.py:194
  639.6 2.2 reduce.18
  642.1 11.4 %all_to_all.118 = bf16[16,2,2048]{2,1,0:T(2,128)(2,1)S(1)} all-to-all(bf16[16,2,2048]{2,1,0:T(2,128)(2,1)S(1)} %reshape.313), channel_id=1, replica_groups=mesh['seq'=16,'head'=8] {'seq'}, dimensions={0} | all-to-all | bytes 262144 | tf_op jit(solution)/shard_map/all_to_all | solution.py:196
  654.9 3.0 fusion.75
  (251 shorter events, 79.0 us)
Async XLA Ops:
  13.2 10.8 %copy-start = (bf16[1,512,1024]{2,1,0:T(8,128)(2,1)S(1)}, bf16[1,512,1024]{2,1,0:T(8,128)(2,1)}, u32[]{:S(2)}) copy-start(bf16[1,512,1024]{2,1,0:T(8,128)(2,1)} %param.20) | copy-start | bytes 3145732
  13.2 375.0 %copy-start.3 = (f32[1024]{0:T(1024)S(1)}, f32[1024]{0:T(1024)}, u32[]{:S(2)}) copy-start(f32[1024]{0:T(1024)} %param.24) | copy-start | bytes 12292
  13.2 375.0 %all-to-all-start = ((bf16[128,8,12288]{2,1,0:T(8,128)(2,1)}), bf16[128,8,12288]{2,1,0:T(8,128)(2,1)}, u32[]{:S(2)}, u32[]{:S(2)}) async-start(bf16[128,8,12288]{2,1,0:T(8,128)(2,1)} %stack.4), calls=%async_computation | async-start | bytes 50331648 | tf_op jit(solution)/shard_map/all_to_all | solution.py:16
  392.5 48.6 %all-to-all-start.2 = ((bf16[1,512,16,64]{1,3,0,2:T(8,128)(2,1)}), bf16[1,512,16,64]{1,3,0,2:T(8,128)(2,1)S(1)}, u32[]{:S(2)}, u32[]{:S(2)}) async-start(bf16[1,512,16,64]{1,3,0,2:T(8,128)(2,1)} %bitcast.26), calls=%async_computation.2 | async-start | bytes 2097152 | tf_op jit(solution)/shard_map/all_to_all | solution.py:160
  426.7 21.3 %copy-start.4 = (f32[1024]{0:T(1024)S(1)}, f32[1024]{0:T(1024)}, u32[]{:S(2)}) copy-start(f32[1024]{0:T(1024)} %param.23) | copy-start | bytes 12292
  441.2 32.7 %all-to-all-start.1 = ((bf16[1,512,16,64]{1,3,0,2:T(8,128)(2,1)}), bf16[1,512,16,64]{1,3,0,2:T(8,128)(2,1)S(1)}, u32[]{:S(2)}, u32[]{:S(2)}) async-start(bf16[1,512,16,64]{1,3,0,2:T(8,128)(2,1)} %bitcast.22), calls=%async_computation.1 | async-start | bytes 2097152 | tf_op jit(solution)/shard_map/all_to_all | solution.py:161
  473.9 1.1 copy-start.1
  476.1 55.0 %copy-start.2 = (f32[2,1024]{1,0:T(2,128)S(1)}, f32[2,1024]{1,0:T(2,128)}, u32[]{:S(2)}) copy-start(f32[2,1024]{1,0:T(2,128)} %param.25) | copy-start | bytes 24580
  523.7 34.8 %all-to-all-start.3 = ((bf16[16,2,2048]{2,1,0:T(2,128)(2,1)}), bf16[16,2,2048]{2,1,0:T(2,128)(2,1)S(1)}, u32[]{:S(2)}, u32[]{:S(2)}) async-start(bf16[16,2,2048]{2,1,0:T(2,128)(2,1)} %reshape.305), calls=%async_computation.3 | async-start | bytes 262144 | tf_op jit(solution)/shard_map/all_to_all | solution.py:183
  593.1 15.7 %all-to-all-start.5 = ((bf16[16,2,2048]{2,1,0:T(2,128)(2,1)}), bf16[16,2,2048]{2,1,0:T(2,128)(2,1)S(1)}, u32[]{:S(2)}, u32[]{:S(2)}) async-start(bf16[16,2,2048]{2,1,0:T(2,128)(2,1)} %reshape.309), calls=%async_computation.5 | async-start | bytes 262144 | tf_op jit(solution)/shard_map/all_to_all | solution.py:196
